TPU v7x, 32 devices: a whole 2x2x4 slice. The times are simulated.
32 devices in a mesh: feat: 8 (over y, x, core), rep: 4 (over z).
Axes of the slice: x: 2, y: 2, z: 4, core: 2. Of those that a mesh axis runs over, the one named last changes fastest.
Arguments:
- features: bfloat16 [4, 8, 1024, 512], P('rep', None, 'feat'), may hold values from -6 to 6
- adjacency_one: int32 [4, 8, 5, 16, 512], P('rep'), may hold values from 0 to 65535, as said below
- pre_hidden: bfloat16 [4, 8, 256, 256], P('rep', 'feat'), may hold values from -6 to 6
- adjacency_two: int32 [4, 8, 5, 8, 256], P('rep', 'feat'), may hold values from 0 to 65535, as said below
- weight_two: bfloat16 [6, 256, 256], replicated, may hold values from -0.375 to 0.375
- out_grad: bfloat16 [4, 8, 128, 256], P('rep', 'feat'), may hold values from -6 to 6
Outputs:
- grad_w1: float32 [6, 1024, 256], P(None, 'feat')
- grad_b1: float32 [256], replicated
- grad_w2: float32 [6, 256, 256], replicated
- grad_b2: float32 [256], replicated
Inputs may be any that keep to these rules, and one draw needn't show every extreme that they name: `adjacency_one`: bit k, k below 16, of word (w, n) is the entry of destination row 16 w + k and source column n; higher bits are zero; some rows are empty. `adjacency_two`: bit k, k below 16, of word (w, n) is the entry of seed row 16 w + k and source column n; higher bits are zero; some rows are empty.
All inputs are finite; a program needn't handle non-finite values.
Results may differ from a plain program's by a relative error of at most 0.0041.
Values may be sent and summed in bfloat16 or wider, within the bound.
No kernel may reach another device: no remote copies, remote signals or barrier semaphores. Data moves between devices by JAX's collectives and lax.ppermute only.
A program may use at most 128 MiB of HBM per device.

v0:
```python
import math
import jax
import jax.numpy as jnp
from jax import lax
from jax.sharding import PartitionSpec as P


def unpack(packed):
    shifts = jnp.arange(16, dtype=jnp.int32)
    spread = jnp.bitwise_and(jnp.right_shift(packed[..., None, :], shifts[:, None]), 1)
    dense = spread.reshape(packed.shape[:-2] + (packed.shape[-2] * 16, packed.shape[-1]))
    degree = jnp.sum(dense, axis=-1).astype(jnp.float32)
    return (dense.astype(jnp.bfloat16), 1.0 / jnp.maximum(degree, 1.0))


def upper_layer(pre_rows, words_two, grad_rows, weight_two, factor):
    hidden = jnp.maximum(pre_rows, 0)
    seed_count = grad_rows.shape[0]
    matrix, inverse = unpack(words_two)
    mixed = (
        jnp.einsum("rsd,dh->rsh", matrix, hidden, preferred_element_type=jnp.float32)
        * inverse[..., None]
    ).astype(jnp.bfloat16)
    scaled = grad_rows.astype(jnp.float32) * factor
    scaled_low = scaled.astype(jnp.bfloat16)
    grad_rel = jnp.einsum("rsh,sk->rhk", mixed, scaled_low, preferred_element_type=jnp.float32)
    grad_self = jnp.einsum(
        "sh,sk->hk", hidden[:seed_count], scaled_low, preferred_element_type=jnp.float32
    )
    weight_grad = jnp.concatenate([grad_self[None], grad_rel], 0)
    backed = (
        jnp.einsum("sk,rhk->rsh", scaled_low, weight_two[1:], preferred_element_type=jnp.float32)
        * inverse[..., None]
    ).astype(jnp.bfloat16)
    spread_back = jnp.einsum("rsd,rsh->dh", matrix, backed, preferred_element_type=jnp.float32)
    own_part = jnp.einsum(
        "sk,hk->sh", scaled_low, weight_two[0], preferred_element_type=jnp.float32
    )
    hidden_total = spread_back + jnp.pad(own_part, ((0, hidden.shape[0] - seed_count), (0, 0)))
    hidden_grad = jnp.where(pre_rows > 0, hidden_total, 0.0).astype(jnp.bfloat16)
    return (
        weight_grad,
        jnp.sum(scaled, 0),
        hidden_grad,
        jnp.sum(hidden_grad.astype(jnp.float32), 0),
    )


def panel_terms(word_block, column_block, grad_block):
    matrix, inverse = unpack(word_block)
    rows_one = grad_block.shape[1]
    gathered = (
        jnp.einsum("brdn,bcn->brdc", matrix, column_block, preferred_element_type=jnp.float32)
        * inverse[..., None]
    ).astype(jnp.bfloat16)
    panel_rel = jnp.einsum(
        "brdc,bdh->rch", gathered, grad_block, preferred_element_type=jnp.float32
    )
    panel_self = jnp.einsum(
        "bcd,bdh->ch", column_block[:, :, :rows_one], grad_block, preferred_element_type=jnp.float32
    )
    return jnp.concatenate([panel_self[None], panel_rel], 0)


def on_device(features, adjacency_one, pre_hidden, adjacency_two, weight_two, out_grad):
    seed_count = out_grad.shape[2]
    factor = float(seed_count * lax.axis_size("feat") * lax.axis_size("rep")) ** (-0.5)
    weight_grad, bias_two, hidden_grad, bias_one = upper_layer(
        pre_hidden[0, 0], adjacency_two[0, 0], out_grad[0, 0], weight_two, factor
    )
    feature_local = features[0]
    adj_local = adjacency_one[0]
    col_width = feature_local.shape[1]
    hidden_width = hidden_grad.shape[1]
    relations = adj_local.shape[1]
    initial = jnp.zeros((relations + 1, col_width, hidden_width), jnp.float32)
    piece = lax.all_gather(hidden_grad[None], "feat", axis=0, tiled=True)
    piece_rows = piece.shape[0]
    group_size = math.gcd(piece_rows, 8)
    turn_count = piece_rows // group_size
    word_block = adj_local
    word_block = word_block.reshape((turn_count, group_size) + adj_local.shape[1:])
    column_block = feature_local
    column_block = column_block.reshape((turn_count, group_size) + feature_local.shape[1:])
    grad_block = piece.reshape((turn_count, group_size) + piece.shape[1:])

    def one_turn(running, inputs):
        return (running + panel_terms(inputs[0], inputs[1], inputs[2]), None)

    running, unused = lax.scan(one_turn, initial, (word_block, column_block, grad_block))
    grad_w1 = lax.psum(running, "rep")
    grad_w2, grad_b1, grad_b2 = lax.psum((weight_grad, bias_one, bias_two), ("feat", "rep"))
    return (grad_w1, grad_b1, grad_w2, grad_b2)


def solution(mesh):
    placed = (
        P("rep", None, "feat", None),
        P("rep", None, None, None, None),
        P("rep", "feat", None, None),
        P("rep", "feat", None, None, None),
        P(),
        P("rep", "feat", None, None),
    )
    return jax.shard_map(
        on_device,
        mesh=mesh,
        in_specs=placed,
        out_specs=(P(None, "feat", None), P(), P(), P()),
        check_vma=False,
    )
```

profile of v0, /device:TPU:0, one launch (start us, length us, event | category | flops | bytes accessed | tf_op | source)
XLA Modules:
  0.0 213.1 jit_solution(5158156742498113044)
XLA Ops:
  8.0 0.0 copy-start
  8.0 0.0 all-gather.3.cloned.1.call-start
  8.1 1.6 fusion.28
  9.7 0.1 div.22
  9.8 0.1 shift_right_arithmetic.72
  9.9 0.9 fusion.27
  10.8 1.1 fusion.37
  11.9 2.4 %convert_reduce_fusion = (f32[256]{0:T(256)S(1)}, bf16[256,256]{1,0:T(8,128)(2,1)}) fusion(f32[128,256]{1,0:T(8,128)S(1)} %fusion.37, bf16[5,128,256]{2,1,0:T(8,128)(2,1)S(1)} %fusion.27, bf16[6,256,256]{2,1,0:T(8,128)(2,1)} %param.10, f32[5,128]{1,0:T(8,128)S(1)} %div.22, bf16[1,1,128,256]{3,2,1,0:T(8,128)(2,1)} %param.11, bf16[1,1,256,256]{3,2,1,0:T(8,128)(2,1)} %param.8), kind=kOutput, calls=%fused_computation.38 | convolution fusion | flops 168722176 | bytes 1445376 | tf_op jit(solution)/shard_map/rsd,rsh->dh/dot_general | solution.py:35
  14.4 0.0 all-gather.3.cloned.1.call-update
  14.4 0.0 all-reduce.7.cloned.1.call-start
  14.4 0.9 broadcast_maximum_fusion
  15.4 1.0 convolution_bitcast_fusion.1
  16.4 1.6 fusion.19
  18.0 1.2 pad_maximum_fusion
  19.3 0.0 all-reduce.7.cloned.1.call-update
  19.3 0.2 all-reduce.5.cloned.1.call-start
  19.5 10.9 %and_reduce_fusion = s32[8,5,16,16]{3,2,1,0:T(8,128)S(1)} fusion(s32[8,5,16,512]{3,2,1,0:T(8,128)S(1)} %bitcast.90), kind=kLoop, calls=%fused_computation.3 | loop fusion | flops 15718400 | bytes 1351680 | tf_op jit(solution)/shard_map/while/body/eval_jaxpr/reduce_sum | solution.py:12
  30.4 0.1 maximum_divide_fusion
  30.5 0.2 reshape.90
  30.7 0.1 shift_right_arithmetic.81
  30.7 10.1 %all-gather.3.cloned.1.call-done = bf16[2048,256]{1,0:T(8,128)(2,1)} async-done(((bf16[256,256]{1,0:T(8,128)(2,1)}), bf16[2048,256]{1,0:T(8,128)(2,1)}) %all-gather.3.cloned.1.call-update) | async-done | bytes 1048592 | tf_op jit(solution)/shard_map/all_gather | solution.py:77
  40.9 10.5 %shift_right_arithmetic.78 = s32[8,5,16,16,512]{4,3,2,1,0:T(8,128)} broadcast(s32[8,5,16,512]{3,2,1,0:T(8,128)S(1)} %bitcast.91), dimensions={0,1,2,4} | broadcast | bytes 22282240 | tf_op jit(solution)/shard_map/while/body/eval_jaxpr/shift_right_arithmetic | solution.py:10
  51.3 9.5 %fusion.13 = f32[5,128,256]{2,1,0:T(8,128)S(1)} fusion(bf16[8,256,256,1]{2,1,0,3:T(8,128)(2,1)S(1)} %bitcast.96, f32[8,5,256]{2,0,1:T(8,128)S(1)} %copy.37, s32[8,5,256,512]{3,2,1,0:T(8,128)} %bitcast.89, s32[256]{0:T(256)S(1)} %shift_right_arithmetic.81, bf16[1,8,128,512]{3,2,1,0:T(8,128)(2,1)S(1)} %copy-done.2), kind=kOutput, calls=%fused_computation.14 | convolution fusion | flops 2031616000 | bytes 23766016 | tf_op jit(solution)/shard_map/while/body/eval_jaxpr/brdc,bdh->rch/dot_general | solution.py:56
  60.8 0.5 convolution_bitcast_fusion.2
  61.3 0.1 copy.30
  61.4 1.0 pad_maximum_fusion.1
  62.4 0.0 all-reduce.5.cloned.1.call-update
  62.4 39.3 %all-reduce.1 = (f32[256]{0:T(256)}, f32[256]{0:T(256)}) all-reduce(f32[256]{0:T(256)S(1)} %get-tuple-element.23, f32[256]{0:T(256)S(1)} %fusion.40), channel_id=1, replica_groups=mesh['feat'=8,'rep'=4] {'feat','rep'}, use_global_device_ids=true, to_apply=%region_4.5 | all-reduce | flops 512 | bytes 4096 | tf_op jit(solution)/shard_map/psum | solution.py:92
  101.8 53.7 %all-reduce.7.cloned.1.call-done = f32[6,256,256]{2,1,0:T(8,128)} async-done(((f32[6,256,256]{2,1,0:T(8,128)}), f32[6,256,256]{2,1,0:T(8,128)}) %all-reduce.7.cloned.1.call-update) | async-done | bytes 1572880 | tf_op jit(solution)/shard_map/psum | solution.py:92
  155.4 45.4 %all-reduce.5.cloned.1.call-done = f32[6,128,256]{2,1,0:T(8,128)} async-done(((f32[6,128,256]{2,1,0:T(8,128)}), f32[6,128,256]{2,1,0:T(8,128)}) %all-reduce.5.cloned.1.call-update) | async-done | bytes 786448 | tf_op jit(solution)/shard_map/psum | solution.py:91
  200.8 2.1 copy.52
  202.9 2.7 %copy.53 = f32[6,256,256]{2,1,0:T(8,128)} copy(f32[6,256,256]{2,1,0:T(8,128)} %all-reduce.7.cloned.1.call-done) | data formatting | bytes 3145728
  (12 shorter events, 0.1 us)
Async XLA Ops:
  8.0 11.5 %copy-start = (s32[1,8,5,16,512]{4,3,2,1,0:T(8,128)S(1)}, s32[1,8,5,16,512]{4,3,2,1,0:T(8,128)}, u32[]{:S(2)}) copy-start(s32[1,8,5,16,512]{4,3,2,1,0:T(8,128)} %param.7) | copy-start | bytes 3932164
  8.0 32.9 %all-gather.3.cloned.1.call-start = ((), (), s32[]{:S(2)}) async-start(), calls=%async_computation.2 | async-start | bytes 1179648 | tf_op jit(solution)/shard_map/all_gather | solution.py:77
  14.4 141.0 %all-reduce.7.cloned.1.call-start = ((), (), s32[]{:S(2)}) async-start(), calls=%async_computation.1 | async-start | bytes 3145728 | tf_op jit(solution)/shard_map/psum | solution.py:92
  19.3 181.5 %all-reduce.5.cloned.1.call-start = ((), (), s32[]{:S(2)}) async-start(), calls=%async_computation | async-start | bytes 1572864 | tf_op jit(solution)/shard_map/psum | solution.py:91
  40.9 10.5 %copy-start.2 = (bf16[1,8,128,512]{3,2,1,0:T(8,128)(2,1)S(1)}, bf16[1,8,128,512]{3,2,1,0:T(8,128)(2,1)}, u32[]{:S(2)}) copy-start(bf16[1,8,128,512]{3,2,1,0:T(8,128)(2,1)} %param.6) | copy-start | bytes 3145732
  40.9 10.5 %copy-start.3 = (bf16[2048,256]{1,0:T(8,128)(2,1)S(1)}, bf16[2048,256]{1,0:T(8,128)(2,1)}, u32[]{:S(2)}) copy-start(bf16[2048,256]{1,0:T(8,128)(2,1)} %all-gather.3.cloned.1.call-done) | copy-start | bytes 3145732
  51.3 11.0 %copy-start.1 = (bf16[1,1,128,256]{3,2,1,0:T(8,128)(2,1)S(1)}, bf16[1,1,128,256]{3,2,1,0:T(8,128)(2,1)}, u32[]{:S(2)}) copy-start(bf16[1,1,128,256]{3,2,1,0:T(8,128)(2,1)} %param.11) | copy-start | bytes 196612
Sparse Core Ops, SparseCore 0:
  14.5 26.3 all-gather.2
Sparse Core Ops, SparseCore 1:
  20.7 134.6 all-reduce.6
  158.2 42.5 all-reduce.4
where the time goes:
time: 214 us; the launch traced here: 213 us
  waiting for transfers between devices  109 us (51%)
  blocking collectives  39.3 us (18%)
  other arithmetic  16.6 us (8%)
  matrix products  16.1 us (8%)
  local copies, waits for them, and re-layouts  15.8 us (7%)
  between operations  15.6 us (7%)
    psum x1, waiting for transfers between devices, on_device(): lax.psum((weight_grad, bias_one, bias_two), ('feat', 'rep'))  53.7 us
    psum x1, waiting for transfers between devices, on_device(): grad_w1 = lax.psum(running, 'rep')  45.4 us
    psum x1, blocking collectives, on_device(): lax.psum((weight_grad, bias_one, bias_two), ('feat', 'rep'))  39.3 us
    reduce_sum x1, other arithmetic, unpack(): degree = jnp.sum(dense, axis=-1).astype(jnp.float32)  10.9 us
    shift_right_arithmetic x5, local copies, waits for them, and re-layouts, unpack(): jnp.right_shift(packed[..., None, :], shifts[:, None])  10.6 us
    all_gather x1, waiting for transfers between devices, on_device(): piece = lax.all_gather(hidden_grad[None], 'feat', axis=0, tiled=True)  10.1 us
    dot_general x1, matrix products, panel_terms(): jnp.einsum('brdc,bdh->rch', gathered, grad_block, preferred_element_type=...  9.46 us
    unnamed x10, local copies, waits for them, and re-layouts  4.85 us
  transfers between devices with their start and end apart: 3, of which 3 were waited for; matrix products, arithmetic and copies ran while one was open for 18% of the time, Pallas kernels for 0%

commit v1 on v0

--- a/solution.py
+++ b/solution.py
@@ -3,6 +3,11 @@
 import jax.numpy as jnp
 from jax import lax
 from jax.sharding import PartitionSpec as P
+
+
+def by_each_axis(array, inner_axis, outer_axis):
+    inner = lax.psum(array, inner_axis)
+    return lax.psum(inner, outer_axis)
 
 
 def unpack(packed):
@@ -89,7 +94,7 @@
 
     running, unused = lax.scan(one_turn, initial, (word_block, column_block, grad_block))
     grad_w1 = lax.psum(running, "rep")
-    grad_w2, grad_b1, grad_b2 = lax.psum((weight_grad, bias_one, bias_two), ("feat", "rep"))
+    grad_w2, grad_b1, grad_b2 = by_each_axis((weight_grad, bias_one, bias_two), "feat", "rep")
     return (grad_w1, grad_b1, grad_w2, grad_b2)
 
 

time: 214 us -> 212 us (level)
  waiting for transfers between devices: 109 us -> 124 us
  blocking collectives: 39.3 us -> 24.9 us
    psum x1, waiting for transfers between devices: 45.4 us -> 72.4 us  [on_device(): grad_w1 = lax.psum(running, 'rep')]
    psum x1 -> x2, blocking collectives: 39.3 us -> 24.9 us  [the longest x1 13.1 us: by_each_axis(): return lax.psum(inner, outer_axis)]
    psum x1, waiting for transfers between devices: 53.7 us -> 41.6 us  [by_each_axis(): inner = lax.psum(array, inner_axis)]
where the time goes in v1:
time: 212 us; the launch traced here: 211 us
  waiting for transfers between devices  124 us (58%)
  blocking collectives  24.9 us (12%)
  other arithmetic  16.7 us (8%)
  matrix products  16.1 us (8%)
  local copies, waits for them, and re-layouts  15.5 us (7%)
  between operations  13.9 us (7%)
    psum x1, waiting for transfers between devices, on_device(): grad_w1 = lax.psum(running, 'rep')  72.4 us
    psum x1, waiting for transfers between devices, by_each_axis(): inner = lax.psum(array, inner_axis)  41.6 us
    psum x1, blocking collectives, by_each_axis(): return lax.psum(inner, outer_axis)  13.1 us
    psum x1, blocking collectives, by_each_axis(): inner = lax.psum(array, inner_axis)  11.8 us
    reduce_sum x1, other arithmetic, unpack(): degree = jnp.sum(dense, axis=-1).astype(jnp.float32)  10.9 us
    shift_right_arithmetic x5, local copies, waits for them, and re-layouts, unpack(): jnp.right_shift(packed[..., None, :], shifts[:, None])  10.3 us
    all_gather x1, waiting for transfers between devices, on_device(): piece = lax.all_gather(hidden_grad[None], 'feat', axis=0, tiled=True)  9.83 us
    dot_general x1, matrix products, panel_terms(): jnp.einsum('brdc,bdh->rch', gathered, grad_block, preferred_element_type=...  9.39 us
  transfers between devices with their start and end apart: 3, of which 3 were waited for; matrix products, arithmetic and copies ran while one was open for 18% of the time, Pallas kernels for 0%

profile of v1, /device:TPU:0, one launch (start us, length us, event | category | flops | bytes accessed | tf_op | source)
XLA Modules:
  0.0 211.1 jit_solution(1814039624088540811)
XLA Ops:
  7.2 0.0 all-gather.3.cloned.1.call-start
  7.2 1.6 fusion.28
  8.9 0.1 div.22
  9.0 0.1 shift_right_arithmetic.72
  9.0 0.9 fusion.27
  10.0 1.1 fusion.37
  11.1 2.4 %convert_reduce_fusion = (f32[256]{0:T(256)S(1)}, bf16[256,256]{1,0:T(8,128)(2,1)}) fusion(f32[128,256]{1,0:T(8,128)S(1)} %fusion.37, bf16[5,128,256]{2,1,0:T(8,128)(2,1)S(1)} %fusion.27, bf16[6,256,256]{2,1,0:T(8,128)(2,1)} %param.10, f32[5,128]{1,0:T(8,128)S(1)} %div.22, bf16[1,1,128,256]{3,2,1,0:T(8,128)(2,1)} %param.11, bf16[1,1,256,256]{3,2,1,0:T(8,128)(2,1)} %param.8), kind=kOutput, calls=%fused_computation.38 | convolution fusion | flops 168722176 | bytes 1445376 | tf_op jit(solution)/shard_map/rsd,rsh->dh/dot_general | solution.py:40
  13.5 0.0 all-gather.3.cloned.1.call-update
  13.6 0.0 all-reduce.7.cloned.1.call-start
  13.6 0.9 broadcast_maximum_fusion
  14.5 1.0 convolution_bitcast_fusion.1
  15.6 1.6 fusion.19
  17.2 1.3 pad_maximum_fusion
  18.5 0.0 all-reduce.7.cloned.1.call-update
  18.5 0.2 all-reduce.9.cloned.1.call-start
  18.8 10.9 %and_reduce_fusion = s32[8,5,16,16]{3,2,1,0:T(8,128)S(1)} fusion(s32[8,5,16,512]{3,2,1,0:T(8,128)S(1)} %bitcast.90), kind=kLoop, calls=%fused_computation.3 | loop fusion | flops 15718400 | bytes 1351680 | tf_op jit(solution)/shard_map/while/body/eval_jaxpr/reduce_sum | solution.py:17
  29.6 0.1 maximum_divide_fusion
  29.7 0.2 reshape.90
  29.9 0.1 shift_right_arithmetic.81
  30.0 9.8 %all-gather.3.cloned.1.call-done = bf16[2048,256]{1,0:T(8,128)(2,1)} async-done(((bf16[256,256]{1,0:T(8,128)(2,1)}), bf16[2048,256]{1,0:T(8,128)(2,1)}) %all-gather.3.cloned.1.call-update) | async-done | bytes 1048592 | tf_op jit(solution)/shard_map/all_gather | solution.py:82
  39.8 10.1 %shift_right_arithmetic.78 = s32[8,5,16,16,512]{4,3,2,1,0:T(8,128)} broadcast(s32[8,5,16,512]{3,2,1,0:T(8,128)S(1)} %bitcast.91), dimensions={0,1,2,4} | broadcast | bytes 22282240 | tf_op jit(solution)/shard_map/while/body/eval_jaxpr/shift_right_arithmetic | solution.py:15
  50.0 9.4 %fusion.13 = f32[5,128,256]{2,1,0:T(8,128)S(1)} fusion(bf16[8,256,256,1]{2,1,0,3:T(8,128)(2,1)S(1)} %bitcast.96, f32[8,5,256]{2,0,1:T(8,128)S(1)} %copy.37, s32[8,5,256,512]{3,2,1,0:T(8,128)} %bitcast.89, s32[256]{0:T(256)S(1)} %shift_right_arithmetic.81, bf16[1,8,128,512]{3,2,1,0:T(8,128)(2,1)S(1)} %copy-done.2), kind=kOutput, calls=%fused_computation.14 | convolution fusion | flops 2031616000 | bytes 23766016 | tf_op jit(solution)/shard_map/while/body/eval_jaxpr/brdc,bdh->rch/dot_general | solution.py:61
  59.4 0.5 convolution_bitcast_fusion.2
  59.8 0.1 copy.30
  59.9 0.9 pad_maximum_fusion.1
  60.9 41.6 %all-reduce.7.cloned.1.call-done = f32[6,256,256]{2,1,0:T(8,128)} async-done(((f32[6,256,256]{2,1,0:T(8,128)}), f32[6,256,256]{2,1,0:T(8,128)}) %all-reduce.7.cloned.1.call-update) | async-done | bytes 1572880 | tf_op jit(solution)/shard_map/psum | solution.py:9
  102.5 0.0 all-reduce.9.cloned.1.call-update
  102.5 11.8 %all-reduce.1 = (f32[256]{0:T(256)S(1)}, f32[256]{0:T(256)S(1)}) all-reduce(f32[256]{0:T(256)S(1)} %get-tuple-element.27, f32[256]{0:T(256)S(1)} %fusion.40), channel_id=1, replica_groups=mesh['feat'=8,'rep'=4] {'feat'}, use_global_device_ids=true, to_apply=%region_4.5 | all-reduce | flops 512 | bytes 4096 | tf_op jit(solution)/shard_map/psum | solution.py:9
  114.3 13.1 %all-reduce.2 = (f32[256]{0:T(256)}, f32[256]{0:T(256)}) all-reduce(f32[256]{0:T(256)S(1)} %get-tuple-element.14, f32[256]{0:T(256)S(1)} %get-tuple-element.20), channel_id=1, replica_groups=mesh['feat'=8,'rep'=4] {'rep'}, use_global_device_ids=true, to_apply=%region_5.6 | all-reduce | flops 512 | bytes 4096 | tf_op jit(solution)/shard_map/psum | solution.py:10
  127.4 72.4 %all-reduce.9.cloned.1.call-done = (f32[6,128,256]{2,1,0:T(8,128)}, f32[6,256,256]{2,1,0:T(8,128)}) async-done(((f32[6,128,256]{2,1,0:T(8,128)}, f32[6,256,256]{2,1,0:T(8,128)}), (f32[6,128,256]{2,1,0:T(8,128)}, f32[6,256,256]{2,1,0:T(8,128)})) %all-reduce.9.cloned.1.call-update) | async-done | bytes 2359312 | tf_op jit(solution)/shard_map/psum | solution.py:96
  199.8 2.1 copy.53
  201.9 2.7 %copy.54 = f32[6,256,256]{2,1,0:T(8,128)} copy(f32[6,256,256]{2,1,0:T(8,128)} %get-tuple-element.31) | data formatting | bytes 3145728
  (13 shorter events, 0.1 us)
Async XLA Ops:
  7.2 32.7 %all-gather.3.cloned.1.call-start = ((), (), s32[]{:S(2)}) async-start(), calls=%async_computation.1 | async-start | bytes 1179648 | tf_op jit(solution)/shard_map/all_gather | solution.py:82
  7.2 11.6 %copy-start = (s32[1,8,5,16,512]{4,3,2,1,0:T(8,128)S(1)}, s32[1,8,5,16,512]{4,3,2,1,0:T(8,128)}, u32[]{:S(2)}) copy-start(s32[1,8,5,16,512]{4,3,2,1,0:T(8,128)} %param.7) | copy-start | bytes 3932164
  13.6 88.9 %all-reduce.7.cloned.1.call-start = ((), (), s32[]{:S(2)}) async-start(), calls=%async_computation | async-start | bytes 3145728 | tf_op jit(solution)/shard_map/psum | solution.py:9
  18.5 181.2 %all-reduce.9.cloned.1.call-start = ((), (), s32[]{:S(2)}) async-start(), calls=%async_computation.2 | async-start | bytes 4718592 | tf_op jit(solution)/shard_map/psum | solution.py:96
  39.8 10.1 %copy-start.2 = (bf16[1,8,128,512]{3,2,1,0:T(8,128)(2,1)S(1)}, bf16[1,8,128,512]{3,2,1,0:T(8,128)(2,1)}, u32[]{:S(2)}) copy-start(bf16[1,8,128,512]{3,2,1,0:T(8,128)(2,1)} %param.6) | copy-start | bytes 3145732
  39.8 10.1 %copy-start.3 = (bf16[2048,256]{1,0:T(8,128)(2,1)S(1)}, bf16[2048,256]{1,0:T(8,128)(2,1)}, u32[]{:S(2)}) copy-start(bf16[2048,256]{1,0:T(8,128)(2,1)} %all-gather.3.cloned.1.call-done) | copy-start | bytes 3145732
  59.4 43.1 %copy-start.1 = (bf16[1,1,128,256]{3,2,1,0:T(8,128)(2,1)S(1)}, bf16[1,1,128,256]{3,2,1,0:T(8,128)(2,1)}, u32[]{:S(2)}) copy-start(bf16[1,1,128,256]{3,2,1,0:T(8,128)(2,1)} %param.11) | copy-start | bytes 196612
Sparse Core Ops, SparseCore 0:
  13.7 26.0 all-gather.2
  43.6 58.7 all-reduce.6
  105.5 94.2 all-reduce.8
